TPU v7x, 256 devices: a whole 4x4x8 slice. The times are simulated.
256 devices in a mesh: bank: 8 (over x, core), zero: 32 (over z, y).
Axes of the slice: x: 4, y: 4, z: 8, core: 2. Of those that a mesh axis runs over, the one named last changes fastest.
Arguments:
- train_gate: float32 [128, 2048, 768], P('bank', 'zero'), may hold values from -0.25 to 0.25
- other_gate: bfloat16 [128, 2048, 768], P('bank', 'zero'), may hold values from -0.0625 to 0.0625
- train_up: float32 [128, 2048, 768], P('bank', 'zero'), may hold values from -0.25 to 0.25
- other_up: bfloat16 [128, 2048, 768], P('bank', 'zero'), may hold values from -0.0625 to 0.0625
- router_weight: float32 [2048, 128], P('zero', 'bank'), may hold values from -0.125 to 0.125
- router_gain: float32 [2048], P('zero'), may hold values from 0.25 to 1.75
Outputs:
- ready_gate: bfloat16 [128, 2048, 768], P('bank', None, 'zero')
- ready_up: bfloat16 [128, 2048, 768], P('bank', None, 'zero')
- scale_gate: float32 [128, 768], P('bank', 'zero')
- scale_up: float32 [128, 768], P('bank', 'zero')
- serve_router: bfloat16 [2048, 128], replicated
All inputs are finite; a program needn't handle non-finite values. Where the computation divides by a largest or mean magnitude, that divisor is 1e-20 or more.
Results may differ from a plain program's by a relative error of at most 0.001.
Values may be sent and summed in bfloat16 or wider, within the bound.
A program may use at most 64 MiB of HBM per device.

v0:
```python
import jax
import jax.numpy as jnp
from jax import lax
from jax.sharding import Mesh
from jax.sharding import PartitionSpec as P

BANK = ("bank_0", "bank_1")


def copy_for_each(x, axis):
    count = lax.axis_size(axis)
    return lax.all_to_all(jnp.broadcast_to(x[None], (count, *x.shape)), axis, 0, 0, tiled=True)


def over_copies(x, axis):
    everything = copy_for_each(x, axis)
    return jnp.max(everything, axis=0)


def in_one(arrays, axis):
    ends = [0]
    for a in arrays:
        ends.append(ends[-1] + a.size)
    subtotal = over_copies(jnp.concatenate([a.ravel() for a in arrays]), axis)
    return tuple((subtotal[b:e].reshape(a.shape) for a, b, e in zip(arrays, ends, ends[1:])))


def in_one_piece(arrays, axis, split_dim, concat_dim, along):
    widths = [a.shape[along] for a in arrays]
    both = jnp.concatenate(arrays, axis=along)
    filled = lax.all_to_all(both, axis, split_axis=split_dim, concat_axis=concat_dim, tiled=True)
    return tuple(jnp.split(filled, [sum(widths[:k]) for k in range(1, len(widths))], axis=along))


def joined_along(blocks, dim):
    shape = list(blocks.shape[1:])
    shape[dim] *= blocks.shape[0]
    return jnp.moveaxis(blocks, 0, dim).reshape(shape)


def collect(x, axis, dim):
    return joined_along(copy_for_each(x, axis), dim)


def edges_of(length, count):
    unit = 8 if length >= 8 * count else 1
    return [length // unit * k // count * unit for k in range(1, count)]


def gather_in_order(x, axes, sequence):
    blocks = x
    for k in sequence:
        blocks = lax.all_gather(blocks, axes[k])
    done = sequence[::-1]
    back = [done.index(k) for k in range(len(axes))]
    blocks = blocks.transpose(*back, *range(len(axes), blocks.ndim))
    return blocks.reshape(-1, *x.shape)


def gather_all_axes(x, axes, dim):
    split_at = max(range(max(1, x.ndim - 1)), key=lambda d: x.shape[d])
    count, gathered = (len(axes), [])
    for initial, piece in enumerate(
        jnp.split(x, edges_of(x.shape[split_at], count), axis=split_at)
    ):
        if piece.size:
            sequence = [(initial - k) % count for k in range(count)]
            gathered.append(gather_in_order(piece, axes, sequence))
    return joined_along(jnp.concatenate(gathered, axis=split_at + 1), dim)


def on_device(train_gate, other_gate, train_up, other_up, router_weight, router_gain):
    latest_gate = train_gate + other_gate.astype(jnp.float32)
    latest_up = train_up + other_up.astype(jnp.float32)
    scale_gate, scale_up = in_one(
        (jnp.max(jnp.abs(latest_gate), axis=1), jnp.max(jnp.abs(latest_up), axis=1)), "zero"
    )
    narrow_gate, narrow_up = (
        (latest_gate / jnp.expand_dims(scale_gate, 1)).astype(jnp.bfloat16),
        (latest_up / jnp.expand_dims(scale_up, 1)).astype(jnp.bfloat16),
    )
    ready_gate, ready_up = in_one_piece((narrow_gate, narrow_up), "zero", 2, 1, 0)
    scale_gate = lax.dynamic_slice_in_dim(
        scale_gate, lax.axis_index("zero") * ready_gate.shape[2], ready_gate.shape[2], axis=1
    )
    scale_up = lax.dynamic_slice_in_dim(
        scale_up, lax.axis_index("zero") * ready_up.shape[2], ready_up.shape[2], axis=1
    )
    part_router = (router_weight * router_gain[:, None]).astype(jnp.bfloat16)
    row_router = collect(part_router, "zero", 0)
    serve_router = gather_all_axes(row_router, BANK, 1)
    return (ready_gate, ready_up, scale_gate, scale_up, serve_router)


def solution(mesh):
    finer = Mesh(mesh.devices.reshape(4, 2, mesh.shape["zero"]), ("bank_0", "bank_1", "zero"))
    return jax.shard_map(
        on_device,
        mesh=finer,
        in_specs=(
            P(BANK, "zero", None),
            P(BANK, "zero", None),
            P(BANK, "zero", None),
            P(BANK, "zero", None),
            P("zero", BANK),
            P("zero"),
        ),
        out_specs=(
            P(BANK, None, "zero"),
            P(BANK, None, "zero"),
            P(BANK, "zero"),
            P(BANK, "zero"),
            P(),
        ),
        check_vma=False,
    )
```

profile of v0, /device:TPU:2, one launch (start us, length us, event | category | flops | bytes accessed | tf_op | source)
XLA Modules:
  0.0 231.7 jit_solution(10446550701950270760)
XLA Ops:
  0.6 0.0 copy-start
  0.6 3.0 %abs_reduce_fusion.1 = f32[16,768]{1,0:T(8,128)S(1)} fusion(f32[16,64,768]{2,1,0:T(8,128)} %param.6, bf16[16,64,768]{2,1,0:T(8,128)(2,1)} %param.7), kind=kLoop, calls=%fused_computation.5 | loop fusion | flops 3133440 | bytes 4767744 | tf_op jit(solution)/shard_map/reduce_max | solution.py:76
  3.7 0.3 copy-done
  3.9 1.9 abs_reduce_fusion
  5.9 4.5 %broadcast_in_dim.4 = f32[32,1,24576]{2,1,0:T(1,128)} broadcast(f32[24576]{0:T(1024)S(1)} %pad_maximum_fusion.2), dimensions={2} | broadcast | bytes 3244032 | tf_op jit(solution)/shard_map/broadcast_in_dim | solution.py:12
  10.3 0.0 copy-start.3
  10.3 0.0 copy-start.4
  10.4 11.6 %all-to-all-start = ((f32[32,1,24576]{2,1,0:T(1,128)}), f32[32,1,24576]{2,1,0:T(1,128)S(1)}, u32[]{:S(2)}, u32[]{:S(2)}) async-start(f32[32,1,24576]{2,1,0:T(1,128)} %broadcast_in_dim.4), calls=%async_computation | async-start | bytes 6291456 | tf_op jit(solution)/shard_map/all_to_all | solution.py:12
  22.0 0.0 copy-done.3
  22.0 0.0 copy-done.4
  22.0 0.8 reshape.74
  22.8 71.5 %all-to-all-done = f32[32,1,24576]{2,1,0:T(1,128)S(1)} async-done(((f32[32,1,24576]{2,1,0:T(1,128)}), f32[32,1,24576]{2,1,0:T(1,128)S(1)}, u32[]{:S(2)}, u32[]{:S(2)}) %all-to-all-start) | async-done | bytes 3145760 | tf_op jit(solution)/shard_map/all_to_all | solution.py:12
  94.3 6.3 %all-to-all-start.2 = ((bf16[32,2,512]{2,1,0:T(2,128)(2,1)}), bf16[32,2,512]{2,1,0:T(2,128)(2,1)S(1)}, u32[]{:S(2)}, u32[]{:S(2)}) async-start(bf16[32,2,512]{2,1,0:T(2,128)(2,1)} %reshape.74), calls=%async_computation.2 | async-start | bytes 131072 | tf_op jit(solution)/shard_map/all_to_all | solution.py:12
  100.6 2.1 reduce_max.29
  102.7 0.0 copy-start.1
  102.7 0.0 copy-start.2
  102.7 4.9 %divide_convert_fusion = (bf16[16,64,768]{2,1,0:T(8,128)(2,1)S(1)}, bf16[16,64,768]{2,1,0:T(8,128)(2,1)S(1)}) fusion(f32[16,64,768]{2,1,0:T(8,128)} %param.8, bf16[16,64,768]{2,1,0:T(8,128)(2,1)} %param.9, f32[16,768]{1,0:T(8,128)S(1)} %slice.37, f32[16,768]{1,0:T(8,128)S(1)} %slice.35, f32[16,64,768]{2,1,0:T(8,128)} %param.6, bf16[16,64,768]{2,1,0:T(8,128)(2,1)} %param.7), kind=kLoop, calls=%fused_computation.1 | loop fusion | flops 6291456 | bytes 12681216 | tf_op jit(solution)/shard_map/convert_element_type | solution.py:80
  107.6 0.0 copy-done.1
  107.6 0.0 copy-done.2
  107.6 0.3 pad_maximum_fusion
  107.9 9.5 %copy.115 = bf16[32,64,768]{1,0,2:T(8,128)(2,1)} copy(bf16[32,64,768]{2,1,0:T(8,128)(2,1)S(1)} %pad_maximum_fusion) | data formatting | bytes 6291456 | tf_op jit(solution)/shard_map/concatenate | solution.py:30
  117.4 8.8 %reshape.72 = bf16[32,2,24576]{2,1,0:T(2,128)(2,1)} reshape(bf16[768,32,64]{2,1,0:T(8,128)(2,1)} %bitcast.28) | data formatting | bytes 6291456
  126.2 0.0 all-to-all-done.2
  126.2 9.8 %all-to-all-start.1 = ((bf16[32,2,24576]{2,1,0:T(2,128)(2,1)}), bf16[32,2,24576]{2,1,0:T(2,128)(2,1)S(1)}, u32[]{:S(2)}, u32[]{:S(2)}) async-start(bf16[32,2,24576]{2,1,0:T(2,128)(2,1)} %reshape.72), calls=%async_computation.1 | async-start | bytes 6291456 | tf_op jit(solution)/shard_map/all_to_all | solution.py:31
  136.0 0.1 reshape.75
  136.2 0.1 all_gather.24
  136.3 12.0 %all_gather.25 = bf16[4,1024,16]{1,2,0:T(8,128)(2,1)S(1)} all-gather(bf16[1,1024,16]{1,2,0:T(8,128)(2,1)S(1)} %all_gather.24), channel_id=1, replica_groups=mesh['bank_0'=4,'bank_1'=2,'zero'=32] {'bank_0'}, dimensions={0}, use_global_device_ids=true | all-gather | bytes 163840 | tf_op jit(solution)/shard_map/all_gather | solution.py:53
  148.3 2.0 all-gather
  150.4 0.1 all_gather.28
  150.5 1.9 all_gather.29
  152.3 12.4 %all-gather.1 = bf16[8,1024,16]{1,2,0:T(8,128)(2,1)S(1)} all-gather(bf16[2,1024,16]{1,2,0:T(8,128)(2,1)S(1)} %all_gather.29), channel_id=3, replica_groups=mesh['bank_0'=4,'bank_1'=2,'zero'=32] {'bank_0'}, dimensions={0}, use_global_device_ids=true | all-gather | bytes 327680 | tf_op jit(solution)/shard_map/all_gather | solution.py:53
  164.8 0.8 pad_maximum_fusion.1
  165.6 2.0 copy.122
  167.6 1.4 constant_dynamic-slice_fusion
  169.1 38.3 %all-to-all-done.1 = bf16[32,2,24576]{2,1,0:T(2,128)(2,1)S(1)} async-done(((bf16[32,2,24576]{2,1,0:T(2,128)(2,1)}), bf16[32,2,24576]{2,1,0:T(2,128)(2,1)S(1)}, u32[]{:S(2)}, u32[]{:S(2)}) %all-to-all-start.1) | async-done | bytes 3145760 | tf_op jit(solution)/shard_map/all_to_all | solution.py:31
  207.4 6.2 %reshape.73 = bf16[768,32,64]{2,1,0:T(8,128)(2,1)} reshape(bf16[32,2,24576]{2,1,0:T(2,128)(2,1)S(1)} %all-to-all-done.1) | data formatting | bytes 6291456
  213.5 5.2 %copy.116 = bf16[32,64,768]{1,2,0:T(8,128)(2,1)S(1)} copy(bf16[32,64,768]{1,0,2:T(8,128)(2,1)} %bitcast.29) | data formatting | bytes 6291456 | tf_op jit(solution)/shard_map/all_to_all | solution.py:31
  218.8 2.7 %fusion = (bf16[16,32,64,24]{2,3,1,0:T(8,128)(2,1)}, bf16[16,32,64,24]{2,3,1,0:T(8,128)(2,1)S(1)}) fusion(bf16[32,32,64,24]{2,3,1,0:T(8,128)(2,1)S(1)} %bitcast.27), kind=kLoop, calls=%fused_computation.12 | loop fusion | bytes 6291456 | tf_op jit(solution)/shard_map/split | solution.py:32
  221.5 0.8 copy.117
  222.3 3.4 %split.17 = bf16[16,2048,24]{1,2,0:T(8,128)(2,1)} reshape(bf16[16,32,64,24]{2,1,3,0:T(8,128)(2,1)S(1)} %copy.117) | data formatting | bytes 3145728 | tf_op jit(solution)/shard_map/split | solution.py:32
  225.7 2.6 %copy.118 = bf16[16,32,64,24]{2,1,3,0:T(8,128)(2,1)S(1)} copy(bf16[16,32,64,24]{2,3,1,0:T(8,128)(2,1)} %get-tuple-element.50) | data formatting | bytes 3145728 | tf_op jit(solution)/shard_map/split | solution.py:32
  228.3 3.4 %split.19 = bf16[16,2048,24]{1,2,0:T(8,128)(2,1)} reshape(bf16[16,32,64,24]{2,1,3,0:T(8,128)(2,1)S(1)} %copy.118) | data formatting | bytes 3145728 | tf_op jit(solution)/shard_map/split | solution.py:32
  (12 shorter events, 0.1 us)
Async XLA Ops:
  0.6 3.3 %copy-start = (f32[16,64,768]{2,1,0:T(8,128)S(1)}, f32[16,64,768]{2,1,0:T(8,128)}, u32[]{:S(2)}) copy-start(f32[16,64,768]{2,1,0:T(8,128)} %param.8) | copy-start | bytes 9437188
  10.3 11.6 %copy-start.3 = (f32[64,16]{0,1:T(8,128)S(1)}, f32[64,16]{0,1:T(8,128)}, u32[]{:S(2)}) copy-start(f32[64,16]{0,1:T(8,128)} %param.10) | copy-start | bytes 12292
  10.3 11.6 %copy-start.4 = (f32[64]{0:T(128)S(1)}, f32[64]{0:T(128)}, u32[]{:S(2)}) copy-start(f32[64]{0:T(128)} %param.11) | copy-start | bytes 772
  10.4 83.9 %all-to-all-start = ((f32[32,1,24576]{2,1,0:T(1,128)}), f32[32,1,24576]{2,1,0:T(1,128)S(1)}, u32[]{:S(2)}, u32[]{:S(2)}) async-start(f32[32,1,24576]{2,1,0:T(1,128)} %broadcast_in_dim.4), calls=%async_computation | async-start | bytes 6291456 | tf_op jit(solution)/shard_map/all_to_all | solution.py:12
  94.3 31.9 %all-to-all-start.2 = ((bf16[32,2,512]{2,1,0:T(2,128)(2,1)}), bf16[32,2,512]{2,1,0:T(2,128)(2,1)S(1)}, u32[]{:S(2)}, u32[]{:S(2)}) async-start(bf16[32,2,512]{2,1,0:T(2,128)(2,1)} %reshape.74), calls=%async_computation.2 | async-start | bytes 131072 | tf_op jit(solution)/shard_map/all_to_all | solution.py:12
  102.7 5.0 %copy-start.1 = (f32[16,768]{1,0:T(8,128)}, f32[16,768]{1,0:T(8,128)S(1)}, u32[]{:S(2)}) copy-start(f32[16,768]{1,0:T(8,128)S(1)} %slice.35) | copy-start | bytes 147460
  102.7 4.9 %copy-start.2 = (f32[16,768]{1,0:T(8,128)}, f32[16,768]{1,0:T(8,128)S(1)}, u32[]{:S(2)}) copy-start(f32[16,768]{1,0:T(8,128)S(1)} %slice.37) | copy-start | bytes 147460
  126.2 81.2 %all-to-all-start.1 = ((bf16[32,2,24576]{2,1,0:T(2,128)(2,1)}), bf16[32,2,24576]{2,1,0:T(2,128)(2,1)S(1)}, u32[]{:S(2)}, u32[]{:S(2)}) async-start(bf16[32,2,24576]{2,1,0:T(2,128)(2,1)} %reshape.72), calls=%async_computation.1 | async-start | bytes 6291456 | tf_op jit(solution)/shard_map/all_to_all | solution.py:31
where the time goes:
time: 233 us; the launch traced here: 232 us
  waiting for transfers between devices  110 us (47%)
  local copies, waits for them, and re-layouts  52 us (22%)
  blocking collectives  28.3 us (12%)
  starting transfers between devices  27.7 us (12%)
  other arithmetic  13 us (6%)
    all_to_all x2, waiting for transfers between devices, copy_for_each(): lax.all_to_all(jnp.broadcast_to(x[None], (count, *x.shape)), axis, 0, 0,...  71.5 us
    all_to_all x1, waiting for transfers between devices, in_one_piece(): lax.all_to_all(both, axis, split_axis=split_dim, concat_axis=concat_dim,...  38.3 us
    all_gather x4, blocking collectives, gather_in_order(): blocks = lax.all_gather(blocks, axes[k])  28.3 us
    unnamed x16, local copies, waits for them, and re-layouts  18.2 us
    all_to_all x2, starting transfers between devices, copy_for_each(): lax.all_to_all(jnp.broadcast_to(x[None], (count, *x.shape)), axis, 0, 0,...  17.9 us
    split x5, local copies, waits for them, and re-layouts, in_one_piece(): jnp.split(filled, [sum(widths[:k]) for k in range(1, len(widths))], axis=...  12.9 us
    all_to_all x1, starting transfers between devices, in_one_piece(): lax.all_to_all(both, axis, split_axis=split_dim, concat_axis=concat_dim,...  9.78 us
    concatenate x1, local copies, waits for them, and re-layouts, in_one_piece(): both = jnp.concatenate(arrays, axis=along)  9.48 us
  transfers between devices with their start and end apart: 3, of which 2 were waited for; matrix products, arithmetic and copies ran while one was open for 13% of the time, Pallas kernels for 0%

commit v1 on v0

v1 whole, which is shorter than its diff:
```python
import functools

import jax
import jax.numpy as jnp
from jax import lax
from jax.experimental import pallas as pl
from jax.experimental.pallas import tpu as pltpu
from jax.sharding import PartitionSpec as P

MESH = pl.DeviceIdType.MESH
PER = 2


def kernel(
    n, nb, ny,
    tg, og, tu, ou, rw, rg,
    out_g, out_u, sc_out, router,
    tgv, ogv, tuv, ouv, part, gath, fin, scales, turned, send, recv, out_gv, out_uv, scv,
    rsend, rrecv, bsend, brecv, routerv,
    in_sem, part_send, part_recv, fin_send, fin_recv, main_send, main_recv,
    r_send, r_recv, b_send, b_recv, out_sem,
):
    experts, rows, cols = tgv.shape
    chunks = experts // PER
    wide = cols // n
    lanes = 2 * rows
    me = lax.axis_index("zero")
    bank = lax.axis_index("bank")
    nz = n // ny
    my_z, my_y = me // ny, me % ny

    def peer_of(k):
        step, dy = k // ny, k % ny
        dz = ((step % 2) * ((step + 1) // 2) + (1 - step % 2) * (nz - step // 2)) % nz
        return ((my_z + dz) % nz) * ny + (my_y + dy) % ny

    def load(c):
        at = pl.ds(c * PER, PER)
        return [
            pltpu.make_async_copy(src.at[at], dst.at[at], in_sem.at[i, c])
            for i, (src, dst) in enumerate(((tg, tgv), (og, ogv), (tu, tuv), (ou, ouv)))
        ]

    for c in range(chunks):
        for copy in load(c):
            copy.start()

    barrier = pltpu.get_barrier_semaphore()

    @pl.loop(1, n)
    def _(k):
        pl.semaphore_signal(barrier, inc=1, device_id={"zero": peer_of(k)}, device_id_type=MESH)

    @pl.loop(1, nb)
    def _(k):
        pl.semaphore_signal(barrier, inc=1, device_id={"bank": (bank + k) % nb}, device_id_type=MESH)

    block = rw[...] * rg[...]
    rsend[...] = jnp.concatenate([block, block], axis=1).astype(jnp.bfloat16)

    @pl.loop(0, chunks)
    def _(c):
        for copy in load(c):
            copy.wait()
        for j in range(PER):
            e = c * PER + j
            for kind, (t, o) in enumerate(((tgv, ogv), (tuv, ouv))):
                latest = t[e] + o[e].astype(jnp.float32)
                part[2 * e + kind] = jnp.max(jnp.abs(latest), axis=0, keepdims=True)

    pl.semaphore_wait(barrier, n - 1 + nb - 1)

    def send_part(row):
        return pltpu.make_async_remote_copy(
            src_ref=part.at[row], dst_ref=gath.at[me], send_sem=part_send, recv_sem=part_recv,
            device_id={"zero": row}, device_id_type=MESH,
        )

    @pl.loop(1, n)
    def _(k):
        send_part(peer_of(k)).start()

    gath[me] = part[me]

    @pl.loop(1, n)
    def _(k):
        pltpu.make_async_remote_copy(
            src_ref=rsend, dst_ref=rrecv.at[me], send_sem=r_send, recv_sem=r_recv,
            device_id={"zero": peer_of(k)}, device_id_type=MESH,
        ).start()

    rrecv[me] = rsend[...]

    pltpu.make_async_copy(gath.at[pl.ds(0, n - 1)], gath.at[pl.ds(0, n - 1)], part_recv).wait()
    total = gath[0]
    for k in range(1, n):
        total = jnp.maximum(total, gath[k])
    fin[0] = total
    scales[me] = total

    @pl.loop(1, n)
    def _(k):
        pltpu.make_async_remote_copy(
            src_ref=fin.at[0], dst_ref=scales.at[me], send_sem=fin_send, recv_sem=fin_recv.at[me],
            device_id={"zero": peer_of(k)}, device_id_type=MESH,
        ).start()

    @pl.loop(0, chunks)
    def _(c):
        for r in range(2 * PER):
            row = c * 2 * PER + r

            @pl.when(row != me)
            def _():
                pltpu.make_async_copy(scales.at[row], scales.at[row], fin_recv.at[row]).wait()

        for j in range(PER):
            e = c * PER + j
            inv_g = 1.0 / scales[2 * e]
            inv_u = 1.0 / scales[2 * e + 1]
            for b in range(cols // 128):
                at = slice(b * 128, (b + 1) * 128)
                gate = (tgv[e, :, at] + ogv[e, :, at].astype(jnp.float32)) * inv_g[:, at]
                up = (tuv[e, :, at] + ouv[e, :, at].astype(jnp.float32)) * inv_u[:, at]
                turned[j, at, :] = jnp.concatenate([gate, up], axis=0).T
        for p in range(n):
            both = jnp.concatenate([turned[j, p * wide : (p + 1) * wide, :] for j in range(PER)], axis=0)
            send[c, p] = both.astype(jnp.bfloat16)
        recv[c, me] = send[c, me]

        @pl.loop(1, n)
        def _(k):
            p = peer_of(k)
            pltpu.make_async_remote_copy(
                src_ref=send.at[c, p], dst_ref=recv.at[c, me], send_sem=main_send.at[c], recv_sem=main_recv.at[c],
                device_id={"zero": p}, device_id_type=MESH,
            ).start()

    pltpu.make_async_copy(rrecv.at[pl.ds(0, n - 1)], rrecv.at[pl.ds(0, n - 1)], r_recv).wait()
    low = lax.broadcasted_iota(jnp.int32, (experts, lanes), 1) < rows

    @pl.loop(0, n // 2)
    def _(k):
        pair = jnp.where(low, rrecv[2 * k].astype(jnp.float32), rrecv[2 * k + 1].astype(jnp.float32))
        bsend[k] = pair.astype(jnp.bfloat16)
        brecv[bank, k] = pair.astype(jnp.bfloat16)

    @pl.loop(1, nb)
    def _(k):
        pltpu.make_async_remote_copy(
            src_ref=bsend, dst_ref=brecv.at[bank], send_sem=b_send, recv_sem=b_recv,
            device_id={"bank": (bank + k) % nb}, device_id_type=MESH,
        ).start()

    table = jnp.concatenate([scales[r] for r in range(2 * experts)], axis=0)
    scv[...] = pltpu.roll(table, (cols - wide * me) % cols, 1)[:, :wide]
    sc_copy = pltpu.make_async_copy(scv, sc_out, out_sem.at[2, 0])
    sc_copy.start()

    pltpu.make_async_copy(brecv.at[pl.ds(0, nb - 1)], brecv.at[pl.ds(0, nb - 1)], b_recv).wait()

    @pl.loop(0, n // 2)
    def _(k):
        tall = jnp.concatenate([brecv[b, k].astype(jnp.float32) for b in range(nb)], axis=0)
        routerv[pl.ds(pl.multiple_of(k * lanes, lanes), lanes), :] = tall.T.astype(jnp.bfloat16)

    router_copy = pltpu.make_async_copy(routerv, router, out_sem.at[2, 1])
    router_copy.start()

    side = lax.broadcasted_iota(jnp.int32, (PER * wide, lanes), 1) < rows

    def store(c):
        at = pl.ds(c * PER, PER)
        return (
            pltpu.make_async_copy(out_gv.at[at], out_g.at[at], out_sem.at[0, c]),
            pltpu.make_async_copy(out_uv.at[at], out_u.at[at], out_sem.at[1, c]),
        )

    @pl.loop(0, chunks)
    def _(c):
        pltpu.make_async_copy(recv.at[c, pl.ds(0, n - 1)], recv.at[c, pl.ds(0, n - 1)], main_recv.at[c]).wait()
        for k in range(n // 2):
            a = recv[c, 2 * k].astype(jnp.float32)
            b = recv[c, 2 * k + 1].astype(jnp.float32)
            gate = jnp.where(side, a, pltpu.roll(b, rows, 1))
            up = jnp.where(side, pltpu.roll(a, rows, 1), b)
            for j in range(PER):
                part_rows = slice(j * wide, (j + 1) * wide)
                out_gv[c * PER + j, :, k * lanes : (k + 1) * lanes] = gate[part_rows].astype(jnp.bfloat16)
                out_uv[c * PER + j, :, k * lanes : (k + 1) * lanes] = up[part_rows].astype(jnp.bfloat16)
        for copy in store(c):
            copy.start()

    pltpu.make_async_copy(part.at[pl.ds(0, n - 1)], part.at[pl.ds(0, n - 1)], part_send).wait()
    pltpu.make_async_copy(scales.at[pl.ds(0, n - 1)], scales.at[pl.ds(0, n - 1)], fin_send).wait()
    pltpu.make_async_copy(rrecv.at[pl.ds(0, n - 1)], rrecv.at[pl.ds(0, n - 1)], r_send).wait()
    pltpu.make_async_copy(brecv.at[pl.ds(0, nb - 1)], brecv.at[pl.ds(0, nb - 1)], b_send).wait()
    for c in range(chunks):
        pltpu.make_async_copy(send.at[c, pl.ds(0, n - 1)], send.at[c, pl.ds(0, n - 1)], main_send.at[c]).wait()
        for copy in store(c):
            copy.wait()
    sc_copy.wait()
    router_copy.wait()


def solution(mesh):
    n, nb = mesh.shape["zero"], mesh.shape["bank"]
    ny = 4

    def on_device(train_gate, other_gate, train_up, other_up, router_weight, router_gain):
        experts, rows, cols = train_gate.shape
        wide, lanes, chunks = cols // n, 2 * rows, experts // PER
        f32, bf16 = jnp.float32, jnp.bfloat16
        hbm, vmem = pl.BlockSpec(memory_space=pl.ANY), pl.BlockSpec(memory_space=pltpu.VMEM)
        dma = pltpu.SemaphoreType.DMA
        out_g, out_u, sc, router = pl.pallas_call(
            functools.partial(kernel, n, nb, ny),
            out_shape=(
                jax.ShapeDtypeStruct((experts, wide, rows * n), bf16),
                jax.ShapeDtypeStruct((experts, wide, rows * n), bf16),
                jax.ShapeDtypeStruct((2 * experts, wide), f32),
                jax.ShapeDtypeStruct((rows * n, experts * nb), bf16),
            ),
            in_specs=[hbm] * 4 + [vmem] * 2,
            out_specs=(hbm,) * 4,
            scratch_shapes=[
                pltpu.VMEM((experts, rows, cols), f32),
                pltpu.VMEM((experts, rows, cols), bf16),
                pltpu.VMEM((experts, rows, cols), f32),
                pltpu.VMEM((experts, rows, cols), bf16),
                pltpu.VMEM((n, 1, cols), f32),
                pltpu.VMEM((n, 1, cols), f32),
                pltpu.VMEM((1, 1, cols), f32),
                pltpu.VMEM((n, 1, cols), f32),
                pltpu.VMEM((PER, cols, lanes), f32),
                pltpu.VMEM((chunks, n, PER * wide, lanes), bf16),
                pltpu.VMEM((chunks, n, PER * wide, lanes), bf16),
                pltpu.VMEM((experts, wide, rows * n), bf16),
                pltpu.VMEM((experts, wide, rows * n), bf16),
                pltpu.VMEM((2 * experts, wide), f32),
                pltpu.VMEM((experts, lanes), bf16),
                pltpu.VMEM((n, experts, lanes), bf16),
                pltpu.VMEM((n // 2, experts, lanes), bf16),
                pltpu.VMEM((nb, n // 2, experts, lanes), bf16),
                pltpu.VMEM((rows * n, experts * nb), bf16),
                dma((4, chunks)),
                dma, dma,
                dma, dma((n,)),
                dma((chunks,)), dma((chunks,)),
                dma, dma,
                dma, dma,
                dma((3, chunks)),
            ],
            compiler_params=pltpu.CompilerParams(
                collective_id=0, has_side_effects=True, vmem_limit_bytes=56 << 20
            ),
        )(train_gate, other_gate, train_up, other_up, router_weight.T, router_gain[None, :])
        scales = sc.reshape(experts, 2, wide)
        return (
            jnp.swapaxes(out_g, 1, 2),
            jnp.swapaxes(out_u, 1, 2),
            scales[:, 0],
            scales[:, 1],
            router,
        )

    return jax.shard_map(
        on_device,
        mesh=mesh,
        in_specs=(
            P("bank", "zero", None),
            P("bank", "zero", None),
            P("bank", "zero", None),
            P("bank", "zero", None),
            P("zero", "bank"),
            P("zero"),
        ),
        out_specs=(
            P("bank", None, "zero"),
            P("bank", None, "zero"),
            P("bank", "zero"),
            P("bank", "zero"),
            P(),
        ),
        check_vma=False,
    )
```

time: 233 us -> 104 us (0.45)
  waiting for transfers between devices: 110 us -> 0 us
  Pallas kernels: 0 us -> 96.8 us
  local copies, waits for them, and re-layouts: 52 us -> 6.45 us
  blocking collectives: 28.3 us -> 0 us
  starting transfers between devices: 27.7 us -> 0 us
  other arithmetic: 13 us -> 0 us
    all_to_all x3 -> x0, waiting for transfers between devices: 110 us -> none  [the longest x2 71.5 us: copy_for_each(): lax.all_to_all(jnp.broadcast_to(x[None], (count, *x.shape)), axis, 0, 0,...]
    pallas_call x0 -> x1, Pallas kernels: none -> 96.8 us  [on_device(): pl.pallas_call(functools.partial(kernel, n, nb, ny), out_shape=(jax.Shape...]
    all_gather x4 -> x0, blocking collectives: 28.3 us -> none  [gather_in_order(): blocks = lax.all_gather(blocks, axes[k])]
    all_to_all x3 -> x0, starting transfers between devices: 27.7 us -> none  [the longest x2 17.9 us: copy_for_each(): lax.all_to_all(jnp.broadcast_to(x[None], (count, *x.shape)), axis, 0, 0,...]
    unnamed x16 -> x7, local copies, waits for them, and re-layouts: 18.2 us -> 5.04 us
    split x8 -> x0, local copies, waits for them, and re-layouts: 12.9 us -> none  [the longest x5 12.9 us: in_one_piece(): jnp.split(filled, [sum(widths[:k]) for k in range(1, len(widths))], axis=...]
    concatenate x1 -> x0, local copies, waits for them, and re-layouts: 9.48 us -> none  [in_one_piece(): both = jnp.concatenate(arrays, axis=along)]
    reduce_max x3 -> x0, other arithmetic: 6.95 us -> none  [the longest x1 2.99 us: on_device(): jnp.max(jnp.abs(latest_gate), axis=1)]
  transfers between devices with their start and end apart: 3 -> 0, of which waited for: 2 -> 0; matrix products, arithmetic and copies ran while one was open for 13% -> 0% of each run, Pallas kernels for 0% -> 0%
where the time goes in v1:
time: 104 us
  Pallas kernels  96.8 us (93%)
  local copies, waits for them, and re-layouts  6.45 us (6%)
    pallas_call x1, Pallas kernels, on_device(): pl.pallas_call(functools.partial(kernel, n, nb, ny), out_shape=(jax.Shape...  96.8 us
    unnamed x7, local copies, waits for them, and re-layouts  5.04 us

profile of v1, /device:TPU:2, one launch (start us, length us, event | category | flops | bytes accessed | tf_op | source)
XLA Modules:
  0.0 103.9 jit_solution(4585126569744107352)
XLA Ops:
  0.6 96.8 %shard_map.101 = (bf16[16,24,2048]{2,1,0:T(8,128)(2,1)}, bf16[16,24,2048]{2,1,0:T(8,128)(2,1)}, f32[32,24]{1,0:T(8,128)}, bf16[2048,128]{1,0:T(8,128)(2,1)}) custom-call(f32[16,64,768]{2,1,0:T(8,128)} %tg.1, bf16[16,64,768]{2,1,0:T(8,128)(2,1)} %og.1, f32[16,64,768]{2,1,0:T(8,128)} %tu.1, bf16[16,64,768]{2,1,0:T(8,128)(2,1)} %ou.1, f32[16,64]{1,0:T(8,128)} %bitcast.16, ...), custom_call_target="tpu_custom_call" | custom-call | tf_op jit(solution)/shard_map/pallas_call | solution.py:216
  97.5 1.4 %fusion = (f32[16,1,24]{2,1,0:T(1,128)}, f32[16,1,24]{2,1,0:T(1,128)}) fusion(f32[16,2,24]{2,1,0:T(2,128)} %bitcast.13), kind=kLoop, calls=%fused_computation | loop fusion | bytes 6144 | tf_op jit(solution)/shard_map/slice | solution.py:263
  98.9 0.0 copy-start
  98.9 2.8 %copy.18 = bf16[16,2048,24]{1,2,0:T(8,128)(2,1)} copy(bf16[16,2048,24]{1,2,0:T(8,128)(2,1)} %bitcast.12) | data formatting | bytes 3145728
  101.7 0.0 copy-done
  101.7 0.0 copy-start.1
  101.7 1.1 %copy.19 = bf16[16,2048,24]{1,2,0:T(8,128)(2,1)} copy(bf16[16,2048,24]{1,2,0:T(8,128)(2,1)S(1)} %bitcast.11) | data formatting | bytes 3145728
  102.9 0.3 copy-done.1
  103.1 0.8 copy.20
Async XLA Ops:
  98.9 2.9 %copy-start = (bf16[16,24,2048]{2,1,0:T(8,128)(2,1)S(1)}, bf16[16,24,2048]{2,1,0:T(8,128)(2,1)}, u32[]{:S(2)}) copy-start(bf16[16,24,2048]{2,1,0:T(8,128)(2,1)} %get-tuple-element.10) | copy-start | bytes 4718596
  101.7 1.4 %copy-start.1 = (bf16[2048,128]{1,0:T(8,128)(2,1)S(1)}, bf16[2048,128]{1,0:T(8,128)(2,1)}, u32[]{:S(2)}) copy-start(bf16[2048,128]{1,0:T(8,128)(2,1)} %get-tuple-element.24) | copy-start | bytes 1572868

commit v2 on v1

v2 whole, which is shorter than its diff:
```python
import functools

import jax
import jax.numpy as jnp
from jax import lax
from jax.experimental import pallas as pl
from jax.experimental.pallas import tpu as pltpu
from jax.sharding import PartitionSpec as P

MESH = pl.DeviceIdType.MESH
PER = 1


def kernel(
    n, nb,
    tg, og, tu, ou, rw, rg,
    out_gv, out_uv, sc_g, sc_u, routerv,
    tgv, ogv, tuv, ouv, rwv, rgv, part, gath, fin, scales, turned, send, recv,
    rsend, rrecv, bsend, brecv,
    in_sem, rw_sem, part_send, part_recv, fin_send, fin_recv, main_send, main_recv,
    r_send, r_recv, b_send, b_recv,
):
    experts, rows, cols = tgv.shape
    chunks = experts // PER
    wide = cols // n
    lanes = 2 * rows
    me = lax.axis_index("zero")
    bank = lax.axis_index("bank")

    def peer_of(k):
        p = me + k
        return jnp.where(p >= n, p - n, p)

    def mate_of(k):
        p = bank + k
        return jnp.where(p >= nb, p - nb, p)

    offsets = sorted(range(1, n), key=lambda k: -min(k, n - k))
    strides = sorted(range(1, nb), key=lambda k: -min(k, nb - k))

    def load(c):
        at = pl.ds(c * PER, PER)
        return [
            pltpu.make_async_copy(src.at[at], dst.at[at], in_sem.at[i, c])
            for i, (src, dst) in enumerate(((tg, tgv), (og, ogv), (tu, tuv), (ou, ouv)))
        ]

    barrier = pltpu.get_barrier_semaphore()

    for k in offsets:
        pl.semaphore_signal(barrier, inc=1, device_id={"zero": peer_of(k)}, device_id_type=MESH)

    for k in strides:
        pl.semaphore_signal(barrier, inc=1, device_id={"bank": mate_of(k)}, device_id_type=MESH)

    for c in range(chunks):
        for copy in load(c):
            copy.start()

    rw_loads = (pltpu.make_async_copy(rw, rwv, rw_sem.at[0]), pltpu.make_async_copy(rg, rgv, rw_sem.at[1]))
    for copy in rw_loads:
        copy.start()

    def send_part(row):
        return pltpu.make_async_remote_copy(
            src_ref=part.at[row], dst_ref=gath.at[me], send_sem=part_send, recv_sem=part_recv,
            device_id={"zero": row}, device_id_type=MESH,
        )

    def largest(c):
        for copy in load(c):
            copy.wait()
        for j in range(PER):
            e = c * PER + j
            for kind, (t, o) in enumerate(((tgv, ogv), (tuv, ouv))):
                latest = t[e] + o[e].astype(jnp.float32)
                part[2 * e + kind] = jnp.max(jnp.abs(latest), axis=0, keepdims=True)

    def pass_on(c):
        for r in range(2 * PER):
            row = c * 2 * PER + r

            @pl.when(row != me)
            def _():
                send_part(row).start()

    largest(0)
    pl.semaphore_wait(barrier, n - 1 + nb - 1)
    pass_on(0)

    @pl.loop(1, chunks)
    def _(c):
        largest(c)
        pass_on(c)

    gath[me] = part[me]

    for copy in rw_loads:
        copy.wait()
    block = rwv[...] * rgv[...]
    rsend[...] = jnp.concatenate([block, block], axis=1).astype(jnp.bfloat16)

    for k in offsets:
        pltpu.make_async_remote_copy(
            src_ref=rsend, dst_ref=rrecv.at[me], send_sem=r_send, recv_sem=r_recv,
            device_id={"zero": peer_of(k)}, device_id_type=MESH,
        ).start()

    rrecv[me] = rsend[...]

    pltpu.make_async_copy(gath.at[pl.ds(0, n - 1)], gath.at[pl.ds(0, n - 1)], part_recv).wait()
    total = gath[0]
    for k in range(1, n):
        total = jnp.maximum(total, gath[k])
    fin[0] = total
    scales[me] = total

    for k in offsets:
        pltpu.make_async_remote_copy(
            src_ref=fin.at[0], dst_ref=scales.at[me], send_sem=fin_send, recv_sem=fin_recv.at[me],
            device_id={"zero": peer_of(k)}, device_id_type=MESH,
        ).start()

    @pl.loop(0, chunks)
    def _(c):
        for r in range(2 * PER):
            row = c * 2 * PER + r

            @pl.when(row != me)
            def _():
                pltpu.make_async_copy(scales.at[row], scales.at[row], fin_recv.at[row]).wait()

        for j in range(PER):
            e = c * PER + j
            inv_g = 1.0 / scales[2 * e]
            inv_u = 1.0 / scales[2 * e + 1]
            for b in range(cols // 128):
                at = slice(b * 128, (b + 1) * 128)
                gate = (tgv[e, :, at] + ogv[e, :, at].astype(jnp.float32)) * inv_g[:, at]
                up = (tuv[e, :, at] + ouv[e, :, at].astype(jnp.float32)) * inv_u[:, at]
                turned[j, at, :] = jnp.concatenate([gate, up], axis=0).T
        for p in range(n):
            both = jnp.concatenate([turned[j, p * wide : (p + 1) * wide, :] for j in range(PER)], axis=0)
            send[c, p] = both.astype(jnp.bfloat16)
        recv[c, me] = send[c, me]

        for k in offsets:
            p = peer_of(k)
            pltpu.make_async_remote_copy(
                src_ref=send.at[c, p], dst_ref=recv.at[c, me], send_sem=main_send.at[c], recv_sem=main_recv.at[c],
                device_id={"zero": p}, device_id_type=MESH,
            ).start()

    pltpu.make_async_copy(rrecv.at[pl.ds(0, n - 1)], rrecv.at[pl.ds(0, n - 1)], r_recv).wait()
    low = lax.broadcasted_iota(jnp.int32, (experts, lanes), 1) < rows

    @pl.loop(0, n // 2)
    def _(k):
        pair = jnp.where(low, rrecv[2 * k].astype(jnp.float32), rrecv[2 * k + 1].astype(jnp.float32))
        bsend[k] = pair.astype(jnp.bfloat16)
        brecv[bank, k] = pair.astype(jnp.bfloat16)

    for k in strides:
        pltpu.make_async_remote_copy(
            src_ref=bsend, dst_ref=brecv.at[bank], send_sem=b_send, recv_sem=b_recv,
            device_id={"bank": mate_of(k)}, device_id_type=MESH,
        ).start()

    for scv, kind in ((sc_g, 0), (sc_u, 1)):
        table = jnp.concatenate([scales[2 * e + kind] for e in range(experts)], axis=0)
        scv[...] = pltpu.roll(table, (cols - wide * me) % cols, 1)[:, :wide]

    pltpu.make_async_copy(brecv.at[pl.ds(0, nb - 1)], brecv.at[pl.ds(0, nb - 1)], b_recv).wait()

    @pl.loop(0, n // 2)
    def _(k):
        tall = jnp.concatenate([brecv[b, k].astype(jnp.float32) for b in range(nb)], axis=0)
        routerv[pl.ds(pl.multiple_of(k * lanes, lanes), lanes), :] = tall.T.astype(jnp.bfloat16)

    side = lax.broadcasted_iota(jnp.int32, (PER * wide, lanes), 1) < rows

    @pl.loop(0, chunks)
    def _(c):
        pltpu.make_async_copy(recv.at[c, pl.ds(0, n - 1)], recv.at[c, pl.ds(0, n - 1)], main_recv.at[c]).wait()
        for k in range(n // 2):
            a = recv[c, 2 * k].astype(jnp.float32)
            b = recv[c, 2 * k + 1].astype(jnp.float32)
            gate = jnp.where(side, a, pltpu.roll(b, rows, 1))
            up = jnp.where(side, pltpu.roll(a, rows, 1), b)
            for j in range(PER):
                part_rows = slice(j * wide, (j + 1) * wide)
                out_gv[c * PER + j, :, k * lanes : (k + 1) * lanes] = gate[part_rows].astype(jnp.bfloat16)
                out_uv[c * PER + j, :, k * lanes : (k + 1) * lanes] = up[part_rows].astype(jnp.bfloat16)

    pltpu.make_async_copy(part.at[pl.ds(0, n - 1)], part.at[pl.ds(0, n - 1)], part_send).wait()
    pltpu.make_async_copy(scales.at[pl.ds(0, n - 1)], scales.at[pl.ds(0, n - 1)], fin_send).wait()
    pltpu.make_async_copy(rrecv.at[pl.ds(0, n - 1)], rrecv.at[pl.ds(0, n - 1)], r_send).wait()
    pltpu.make_async_copy(brecv.at[pl.ds(0, nb - 1)], brecv.at[pl.ds(0, nb - 1)], b_send).wait()
    for c in range(chunks):
        pltpu.make_async_copy(send.at[c, pl.ds(0, n - 1)], send.at[c, pl.ds(0, n - 1)], main_send.at[c]).wait()


def store(*refs):
    arrays = len(refs) // 2
    ins, outs, sem = refs[:arrays], refs[arrays : 2 * arrays], refs[-1]
    copies = [pltpu.make_async_copy(i, o, sem.at[k]) for k, (i, o) in enumerate(zip(ins, outs))]
    for copy in copies:
        copy.start()
    for copy in copies:
        copy.wait()


def solution(mesh):
    n, nb = mesh.shape["zero"], mesh.shape["bank"]

    def on_device(train_gate, other_gate, train_up, other_up, router_weight, router_gain):
        experts, rows, cols = train_gate.shape
        wide, lanes, chunks = cols // n, 2 * rows, experts // PER
        f32, bf16 = jnp.float32, jnp.bfloat16
        hbm, vmem = pl.BlockSpec(memory_space=pltpu.HBM), pl.BlockSpec(memory_space=pltpu.VMEM)
        dma = pltpu.SemaphoreType.DMA
        shapes = (
            jax.ShapeDtypeStruct((experts, wide, rows * n), bf16),
            jax.ShapeDtypeStruct((experts, wide, rows * n), bf16),
            jax.ShapeDtypeStruct((experts, wide), f32),
            jax.ShapeDtypeStruct((experts, wide), f32),
            jax.ShapeDtypeStruct((rows * n, experts * nb), bf16),
        )
        held = pl.pallas_call(
            functools.partial(kernel, n, nb),
            out_shape=tuple(pltpu.VMEM(a.shape, a.dtype) for a in shapes),
            in_specs=[hbm] * 6,
            out_specs=(vmem,) * 5,
            scratch_shapes=[
                pltpu.VMEM((experts, rows, cols), f32),
                pltpu.VMEM((experts, rows, cols), bf16),
                pltpu.VMEM((experts, rows, cols), f32),
                pltpu.VMEM((experts, rows, cols), bf16),
                pltpu.VMEM((experts, rows), f32),
                pltpu.VMEM((1, rows), f32),
                pltpu.VMEM((n, 1, cols), f32),
                pltpu.VMEM((n, 1, cols), f32),
                pltpu.VMEM((1, 1, cols), f32),
                pltpu.VMEM((n, 1, cols), f32),
                pltpu.VMEM((PER, cols, lanes), f32),
                pltpu.VMEM((chunks, n, PER * wide, lanes), bf16),
                pltpu.VMEM((chunks, n, PER * wide, lanes), bf16),
                pltpu.VMEM((experts, lanes), bf16),
                pltpu.VMEM((n, experts, lanes), bf16),
                pltpu.VMEM((n // 2, experts, lanes), bf16),
                pltpu.VMEM((nb, n // 2, experts, lanes), bf16),
                dma((4, chunks)),
                dma((2,)),
                dma, dma,
                dma, dma((n,)),
                dma((chunks,)), dma((chunks,)),
                dma, dma,
                dma, dma,
            ],
            compiler_params=pltpu.CompilerParams(
                collective_id=0, has_side_effects=True, vmem_limit_bytes=40 << 20
            ),
        )(
            *(
                pltpu.with_memory_space_constraint(a, pltpu.HBM)
                for a in (train_gate, other_gate, train_up, other_up, router_weight.T, router_gain[None, :])
            )
        )
        out_g, out_u, sc_g, sc_u, router = pl.pallas_call(
            store,
            out_shape=shapes,
            in_specs=[vmem] * 5,
            out_specs=(hbm,) * 5,
            scratch_shapes=[dma((5,))],
            compiler_params=pltpu.CompilerParams(vmem_limit_bytes=4 << 20),
        )(*held)
        return jnp.swapaxes(out_g, 1, 2), jnp.swapaxes(out_u, 1, 2), sc_g, sc_u, router

    return jax.shard_map(
        on_device,
        mesh=mesh,
        in_specs=(
            P("bank", "zero", None),
            P("bank", "zero", None),
            P("bank", "zero", None),
            P("bank", "zero", None),
            P("zero", "bank"),
            P("zero"),
        ),
        out_specs=(
            P("bank", None, "zero"),
            P("bank", None, "zero"),
            P("bank", "zero"),
            P("bank", "zero"),
            P(),
        ),
        check_vma=False,
    )
```

time: 104 us -> 95.9 us (0.922)
  local copies, waits for them, and re-layouts: 6.45 us -> 0 us
  Pallas kernels: 96.8 us -> 94.3 us
    unnamed x7 -> x0, local copies, waits for them, and re-layouts: 5.04 us -> none
    pallas_call x1 -> x2, Pallas kernels: 96.8 us -> 94.3 us  [the longest x1 92.4 us: on_device(): pl.pallas_call(functools.partial(kernel, n, nb), out_shape=tuple((pltpu.V...]
    slice x1 -> x0, local copies, waits for them, and re-layouts: 1.41 us -> none  [on_device(): scales[:, 1]]
where the time goes in v2:
time: 95.9 us; the launch traced here: 95 us
  Pallas kernels  94.3 us (98%)
    pallas_call x1, Pallas kernels, on_device(): pl.pallas_call(functools.partial(kernel, n, nb), out_shape=tuple((pltpu.V...  92.4 us

profile of v2, /device:TPU:2, one launch (start us, length us, event | category | flops | bytes accessed | tf_op | source)
XLA Modules:
  0.0 95.0 jit_solution(13734071117593417670)
XLA Ops:
  0.6 92.4 %shard_map.101 = (bf16[16,24,2048]{2,1,0:T(8,128)(2,1)S(1)}, bf16[16,24,2048]{2,1,0:T(8,128)(2,1)S(1)}, f32[16,24]{1,0:T(8,128)S(1)}, f32[16,24]{1,0:T(8,128)S(1)}, bf16[2048,128]{1,0:T(8,128)(2,1)S(1)}) custom-call(f32[16,64,768]{2,1,0:T(8,128)} %tg.1, bf16[16,64,768]{2,1,0:T(8,128)(2,1)} %og.1, f32[16,64,768]{2,1,0:T(8,128)} %tu.1, ...), custom_call_target="tpu_custom_call" | custom-call | tf_op jit(solution)/shard_map/pallas_call | solution.py:229
  93.1 1.9 %shard_map.102 = (bf16[16,24,2048]{2,1,0:T(8,128)(2,1)}, bf16[16,24,2048]{2,1,0:T(8,128)(2,1)}, f32[16,24]{1,0:T(8,128)}, f32[16,24]{1,0:T(8,128)}, bf16[2048,128]{1,0:T(8,128)(2,1)}) custom-call(bf16[16,24,2048]{2,1,0:T(8,128)(2,1)S(1)} %get-tuple-element.15.refs_0_, bf16[16,24,2048]{2,1,0:T(8,128)(2,1)S(1)} %get-tuple-element.16.refs_1_, ...), custom_call_target="tpu_custom_call" | custom-call | tf_op jit(solution)/shard_map/pallas_call | solution.py:269

commit v3 on v2

--- a/solution.py
+++ b/solution.py
@@ -24,6 +24,7 @@
     chunks = experts // PER
     wide = cols // n
     lanes = 2 * rows
+    half = experts // 2
     me = lax.axis_index("zero")
     bank = lax.axis_index("bank")
 
@@ -98,7 +99,7 @@
     for copy in rw_loads:
         copy.wait()
     block = rwv[...] * rgv[...]
-    rsend[...] = jnp.concatenate([block, block], axis=1).astype(jnp.bfloat16)
+    rsend[...] = jnp.concatenate([block[:half], block[half:]], axis=1).astype(jnp.bfloat16)
 
     for k in offsets:
         pltpu.make_async_remote_copy(
@@ -152,13 +153,17 @@
             ).start()
 
     pltpu.make_async_copy(rrecv.at[pl.ds(0, n - 1)], rrecv.at[pl.ds(0, n - 1)], r_recv).wait()
-    low = lax.broadcasted_iota(jnp.int32, (experts, lanes), 1) < rows
+    low = lax.broadcasted_iota(jnp.int32, (half, lanes), 1) < rows
 
     @pl.loop(0, n // 2)
     def _(k):
-        pair = jnp.where(low, rrecv[2 * k].astype(jnp.float32), rrecv[2 * k + 1].astype(jnp.float32))
-        bsend[k] = pair.astype(jnp.bfloat16)
-        brecv[bank, k] = pair.astype(jnp.bfloat16)
+        a = rrecv[2 * k].astype(jnp.float32)
+        b = rrecv[2 * k + 1].astype(jnp.float32)
+        first = jnp.where(low, a, pltpu.roll(b, rows, 1))
+        second = jnp.where(low, pltpu.roll(a, rows, 1), b)
+        pair = jnp.concatenate([first, second], axis=0).astype(jnp.bfloat16)
+        bsend[k] = pair
+        brecv[bank, k] = pair
 
     for k in strides:
         pltpu.make_async_remote_copy(
@@ -245,8 +250,8 @@
                 pltpu.VMEM((PER, cols, lanes), f32),
                 pltpu.VMEM((chunks, n, PER * wide, lanes), bf16),
                 pltpu.VMEM((chunks, n, PER * wide, lanes), bf16),
-                pltpu.VMEM((experts, lanes), bf16),
-                pltpu.VMEM((n, experts, lanes), bf16),
+                pltpu.VMEM((experts // 2, lanes), bf16),
+                pltpu.VMEM((n, experts // 2, lanes), bf16),
                 pltpu.VMEM((n // 2, experts, lanes), bf16),
                 pltpu.VMEM((nb, n // 2, experts, lanes), bf16),
                 dma((4, chunks)),

time: 95.9 us -> 94.4 us (0.984)
  no operation moved by 1% of the time
where the time goes in v3:
time: 94.4 us; the launch traced here: 94.2 us
  Pallas kernels  93.5 us (99%)
    pallas_call x1, Pallas kernels, on_device(): pl.pallas_call(functools.partial(kernel, n, nb), out_shape=tuple((pltpu.V...  91.7 us

profile of v3, /device:TPU:2, one launch (start us, length us, event | category | flops | bytes accessed | tf_op | source)
XLA Modules:
  0.0 94.2 jit_solution(8481961042876471923)
XLA Ops:
  0.6 91.7 %shard_map.101 = (bf16[16,24,2048]{2,1,0:T(8,128)(2,1)S(1)}, bf16[16,24,2048]{2,1,0:T(8,128)(2,1)S(1)}, f32[16,24]{1,0:T(8,128)S(1)}, f32[16,24]{1,0:T(8,128)S(1)}, bf16[2048,128]{1,0:T(8,128)(2,1)S(1)}) custom-call(f32[16,64,768]{2,1,0:T(8,128)} %tg.1, bf16[16,64,768]{2,1,0:T(8,128)(2,1)} %og.1, f32[16,64,768]{2,1,0:T(8,128)} %tu.1, ...), custom_call_target="tpu_custom_call" | custom-call | tf_op jit(solution)/shard_map/pallas_call | solution.py:234
  92.3 1.9 %shard_map.102 = (bf16[16,24,2048]{2,1,0:T(8,128)(2,1)}, bf16[16,24,2048]{2,1,0:T(8,128)(2,1)}, f32[16,24]{1,0:T(8,128)}, f32[16,24]{1,0:T(8,128)}, bf16[2048,128]{1,0:T(8,128)(2,1)}) custom-call(bf16[16,24,2048]{2,1,0:T(8,128)(2,1)S(1)} %get-tuple-element.15.refs_0_, bf16[16,24,2048]{2,1,0:T(8,128)(2,1)S(1)} %get-tuple-element.16.refs_1_, ...), custom_call_target="tpu_custom_call" | custom-call | tf_op jit(solution)/shard_map/pallas_call | solution.py:274

commit v4 on v3

--- a/solution.py
+++ b/solution.py
@@ -8,7 +8,7 @@
 from jax.sharding import PartitionSpec as P
 
 MESH = pl.DeviceIdType.MESH
-PER = 1
+NY = 4
 
 
 def kernel(
@@ -17,35 +17,48 @@
     out_gv, out_uv, sc_g, sc_u, routerv,
     tgv, ogv, tuv, ouv, rwv, rgv, part, gath, fin, scales, turned, send, recv,
     rsend, rrecv, bsend, brecv,
-    in_sem, rw_sem, part_send, part_recv, fin_send, fin_recv, main_send, main_recv,
+    in_sem, rw_sem, part_send, part_recv, fin_send, fin_recv, side_send, side_recv, main_send, main_recv,
     r_send, r_recv, b_send, b_recv,
 ):
     experts, rows, cols = tgv.shape
-    chunks = experts // PER
+    chunks = experts
     wide = cols // n
     lanes = 2 * rows
     half = experts // 2
     me = lax.axis_index("zero")
     bank = lax.axis_index("bank")
 
-    def peer_of(k):
-        p = me + k
-        return jnp.where(p >= n, p - n, p)
-
     def mate_of(k):
         p = bank + k
         return jnp.where(p >= nb, p - nb, p)
 
-    offsets = sorted(range(1, n), key=lambda k: -min(k, n - k))
+    my_z = lax.div(me, NY)
+    my_y = me - my_z * NY
+    nz = n // NY
+
+    def peer_of(k):
+        z, y = my_z + k // NY, my_y + k % NY
+        return jnp.where(z >= nz, z - nz, z) * NY + jnp.where(y >= NY, y - NY, y)
+
+    def place(r):
+        return r % NY * nz + r // NY
+
+    def hops(k):
+        return min(k // NY, nz - k // NY), min(k % NY, NY - k % NY)
+
+    offsets = sorted(range(1, n), key=lambda k: (-hops(k)[0], -hops(k)[1]))
     strides = sorted(range(1, nb), key=lambda k: -min(k, nb - k))
 
     def load(c):
-        at = pl.ds(c * PER, PER)
+        at = pl.ds(c, 1)
         return [
             pltpu.make_async_copy(src.at[at], dst.at[at], in_sem.at[i, c])
             for i, (src, dst) in enumerate(((tg, tgv), (og, ogv), (tu, tuv), (ou, ouv)))
         ]
 
+    for copy in load(0):
+        copy.start()
+
     barrier = pltpu.get_barrier_semaphore()
 
     for k in offsets:
@@ -54,7 +67,7 @@
     for k in strides:
         pl.semaphore_signal(barrier, inc=1, device_id={"bank": mate_of(k)}, device_id_type=MESH)
 
-    for c in range(chunks):
+    for c in range(1, chunks):
         for copy in load(c):
             copy.start()
 
@@ -71,15 +84,12 @@
     def largest(c):
         for copy in load(c):
             copy.wait()
-        for j in range(PER):
-            e = c * PER + j
-            for kind, (t, o) in enumerate(((tgv, ogv), (tuv, ouv))):
-                latest = t[e] + o[e].astype(jnp.float32)
-                part[2 * e + kind] = jnp.max(jnp.abs(latest), axis=0, keepdims=True)
+        for kind, (t, o) in enumerate(((tgv, ogv), (tuv, ouv))):
+            latest = t[c] + o[c].astype(jnp.float32)
+            part[2 * c + kind] = jnp.max(jnp.abs(latest), axis=0, keepdims=True)
 
     def pass_on(c):
-        for r in range(2 * PER):
-            row = c * 2 * PER + r
+        for row in (2 * c, 2 * c + 1):
 
             @pl.when(row != me)
             def _():
@@ -114,43 +124,77 @@
     for k in range(1, n):
         total = jnp.maximum(total, gath[k])
     fin[0] = total
-    scales[me] = total
-
-    for k in offsets:
-        pltpu.make_async_remote_copy(
-            src_ref=fin.at[0], dst_ref=scales.at[me], send_sem=fin_send, recv_sem=fin_recv.at[me],
-            device_id={"zero": peer_of(k)}, device_id_type=MESH,
-        ).start()
-
-    @pl.loop(0, chunks)
-    def _(c):
-        for r in range(2 * PER):
-            row = c * 2 * PER + r
-
-            @pl.when(row != me)
-            def _():
-                pltpu.make_async_copy(scales.at[row], scales.at[row], fin_recv.at[row]).wait()
-
-        for j in range(PER):
-            e = c * PER + j
-            inv_g = 1.0 / scales[2 * e]
-            inv_u = 1.0 / scales[2 * e + 1]
-            for b in range(cols // 128):
-                at = slice(b * 128, (b + 1) * 128)
-                gate = (tgv[e, :, at] + ogv[e, :, at].astype(jnp.float32)) * inv_g[:, at]
-                up = (tuv[e, :, at] + ouv[e, :, at].astype(jnp.float32)) * inv_u[:, at]
-                turned[j, at, :] = jnp.concatenate([gate, up], axis=0).T
+    scales[my_y * nz + my_z] = total
+
+    def send_fin(peer):
+        return pltpu.make_async_remote_copy(
+            src_ref=fin.at[0], dst_ref=scales.at[my_y * nz + my_z], send_sem=fin_send, recv_sem=fin_recv.at[me],
+            device_id={"zero": peer}, device_id_type=MESH,
+        )
+
+    @pl.when(my_z == 0)
+    def _():
+        for k in offsets:
+            send_fin(peer_of(k)).start()
+
+    @pl.when(my_z > 0)
+    def _():
+        for k in sorted(range(1, nz), key=lambda k: -min(k, nz - k)):
+            send_fin(peer_of(k * NY)).start()
+
+    def take_fin(row, at):
+        pltpu.make_async_copy(scales.at[at], scales.at[at], fin_recv.at[row]).wait()
+
+    for r in range(NY):
+
+        @pl.when(me != r)
+        def _():
+            take_fin(r, place(r))
+
+    def post(c):
+        y, z = lax.rem(2 * c, NY), lax.div(2 * c, NY)
+        inv_g = 1.0 / scales[y * nz + z]
+        inv_u = 1.0 / scales[(y + 1) * nz + z]
+        for b in range(cols // 128):
+            at = slice(b * 128, (b + 1) * 128)
+            gate = (tgv[c, :, at] + ogv[c, :, at].astype(jnp.float32)) * inv_g[:, at]
+            up = (tuv[c, :, at] + ouv[c, :, at].astype(jnp.float32)) * inv_u[:, at]
+            turned[at, :] = jnp.concatenate([gate, up], axis=0).T
         for p in range(n):
-            both = jnp.concatenate([turned[j, p * wide : (p + 1) * wide, :] for j in range(PER)], axis=0)
-            send[c, p] = both.astype(jnp.bfloat16)
+            send[c, p] = turned[p * wide : (p + 1) * wide, :].astype(jnp.bfloat16)
         recv[c, me] = send[c, me]
-
         for k in offsets:
             p = peer_of(k)
             pltpu.make_async_remote_copy(
                 src_ref=send.at[c, p], dst_ref=recv.at[c, me], send_sem=main_send.at[c], recv_sem=main_recv.at[c],
                 device_id={"zero": p}, device_id_type=MESH,
             ).start()
+
+    def send_rows(k):
+        at = pl.ds(my_y * nz + 1, nz - 1)
+        return pltpu.make_async_remote_copy(
+            src_ref=scales.at[at], dst_ref=scales.at[at], send_sem=side_send, recv_sem=side_recv.at[my_y],
+            device_id={"zero": peer_of(k)}, device_id_type=MESH,
+        )
+
+    post(0)
+    for z in range(1, nz):
+
+        @pl.when(my_z != z)
+        def _():
+            take_fin(z * NY + my_y, my_y * nz + z)
+
+    for k in range(1, NY):
+        send_rows(k).start()
+    post(1)
+    for y in range(NY):
+
+        @pl.when(my_y != y)
+        def _():
+            at = pl.ds(y * nz + 1, nz - 1)
+            pltpu.make_async_copy(scales.at[at], scales.at[at], side_recv.at[y]).wait()
+
+    pl.loop(2, chunks)(post)
 
     pltpu.make_async_copy(rrecv.at[pl.ds(0, n - 1)], rrecv.at[pl.ds(0, n - 1)], r_recv).wait()
     low = lax.broadcasted_iota(jnp.int32, (half, lanes), 1) < rows
@@ -172,7 +216,7 @@
         ).start()
 
     for scv, kind in ((sc_g, 0), (sc_u, 1)):
-        table = jnp.concatenate([scales[2 * e + kind] for e in range(experts)], axis=0)
+        table = jnp.concatenate([scales[place(2 * e + kind)] for e in range(experts)], axis=0)
         scv[...] = pltpu.roll(table, (cols - wide * me) % cols, 1)[:, :wide]
 
     pltpu.make_async_copy(brecv.at[pl.ds(0, nb - 1)], brecv.at[pl.ds(0, nb - 1)], b_recv).wait()
@@ -182,7 +226,7 @@
         tall = jnp.concatenate([brecv[b, k].astype(jnp.float32) for b in range(nb)], axis=0)
         routerv[pl.ds(pl.multiple_of(k * lanes, lanes), lanes), :] = tall.T.astype(jnp.bfloat16)
 
-    side = lax.broadcasted_iota(jnp.int32, (PER * wide, lanes), 1) < rows
+    side = lax.broadcasted_iota(jnp.int32, (wide, lanes), 1) < rows
 
     @pl.loop(0, chunks)
     def _(c):
@@ -192,13 +236,21 @@
             b = recv[c, 2 * k + 1].astype(jnp.float32)
             gate = jnp.where(side, a, pltpu.roll(b, rows, 1))
             up = jnp.where(side, pltpu.roll(a, rows, 1), b)
-            for j in range(PER):
-                part_rows = slice(j * wide, (j + 1) * wide)
-                out_gv[c * PER + j, :, k * lanes : (k + 1) * lanes] = gate[part_rows].astype(jnp.bfloat16)
-                out_uv[c * PER + j, :, k * lanes : (k + 1) * lanes] = up[part_rows].astype(jnp.bfloat16)
+            out_gv[c, :, k * lanes : (k + 1) * lanes] = gate.astype(jnp.bfloat16)
+            out_uv[c, :, k * lanes : (k + 1) * lanes] = up.astype(jnp.bfloat16)
 
     pltpu.make_async_copy(part.at[pl.ds(0, n - 1)], part.at[pl.ds(0, n - 1)], part_send).wait()
-    pltpu.make_async_copy(scales.at[pl.ds(0, n - 1)], scales.at[pl.ds(0, n - 1)], fin_send).wait()
+
+    @pl.when(my_z == 0)
+    def _():
+        pltpu.make_async_copy(scales.at[pl.ds(0, n - 1)], scales.at[pl.ds(0, n - 1)], fin_send).wait()
+
+    @pl.when(my_z > 0)
+    def _():
+        pltpu.make_async_copy(scales.at[pl.ds(0, nz - 1)], scales.at[pl.ds(0, nz - 1)], fin_send).wait()
+
+    sides = pl.ds(0, (NY - 1) * (nz - 1))
+    pltpu.make_async_copy(scales.at[sides], scales.at[sides], side_send).wait()
     pltpu.make_async_copy(rrecv.at[pl.ds(0, n - 1)], rrecv.at[pl.ds(0, n - 1)], r_send).wait()
     pltpu.make_async_copy(brecv.at[pl.ds(0, nb - 1)], brecv.at[pl.ds(0, nb - 1)], b_send).wait()
     for c in range(chunks):
@@ -220,7 +272,7 @@
 
     def on_device(train_gate, other_gate, train_up, other_up, router_weight, router_gain):
         experts, rows, cols = train_gate.shape
-        wide, lanes, chunks = cols // n, 2 * rows, experts // PER
+        wide, lanes, chunks = cols // n, 2 * rows, experts
         f32, bf16 = jnp.float32, jnp.bfloat16
         hbm, vmem = pl.BlockSpec(memory_space=pltpu.HBM), pl.BlockSpec(memory_space=pltpu.VMEM)
         dma = pltpu.SemaphoreType.DMA
@@ -247,9 +299,9 @@
                 pltpu.VMEM((n, 1, cols), f32),
                 pltpu.VMEM((1, 1, cols), f32),
                 pltpu.VMEM((n, 1, cols), f32),
-                pltpu.VMEM((PER, cols, lanes), f32),
-                pltpu.VMEM((chunks, n, PER * wide, lanes), bf16),
-                pltpu.VMEM((chunks, n, PER * wide, lanes), bf16),
+                pltpu.VMEM((cols, lanes), f32),
+                pltpu.VMEM((chunks, n, wide, lanes), bf16),
+                pltpu.VMEM((chunks, n, wide, lanes), bf16),
                 pltpu.VMEM((experts // 2, lanes), bf16),
                 pltpu.VMEM((n, experts // 2, lanes), bf16),
                 pltpu.VMEM((n // 2, experts, lanes), bf16),
@@ -258,6 +310,7 @@
                 dma((2,)),
                 dma, dma,
                 dma, dma((n,)),
+                dma, dma((NY,)),
                 dma((chunks,)), dma((chunks,)),
                 dma, dma,
                 dma, dma,

time: 94.4 us -> 93.2 us (0.987)
  Pallas kernels: 93.5 us -> 92.3 us
    pallas_call x1, Pallas kernels: 91.7 us -> 90.4 us  [on_device(): pl.pallas_call(functools.partial(kernel, n, nb), out_shape=tuple((pltpu.V...]
where the time goes in v4:
time: 93.2 us; the launch traced here: 92.9 us
  Pallas kernels  92.3 us (99%)
    pallas_call x1, Pallas kernels, on_device(): pl.pallas_call(functools.partial(kernel, n, nb), out_shape=tuple((pltpu.V...  90.4 us
    pallas_call x1, Pallas kernels, on_device(): pl.pallas_call(store, out_shape=shapes, in_specs=[vmem] * 5, out_specs=(h...  1.88 us

profile of v4, /device:TPU:2, one launch (start us, length us, event | category | flops | bytes accessed | tf_op | source)
XLA Modules:
  0.0 92.9 jit_solution(196603445118791575)
XLA Ops:
  0.6 90.4 %shard_map.101 = (bf16[16,24,2048]{2,1,0:T(8,128)(2,1)S(1)}, bf16[16,24,2048]{2,1,0:T(8,128)(2,1)S(1)}, f32[16,24]{1,0:T(8,128)S(1)}, f32[16,24]{1,0:T(8,128)S(1)}, bf16[2048,128]{1,0:T(8,128)(2,1)S(1)}) custom-call(f32[16,64,768]{2,1,0:T(8,128)} %tg.1, bf16[16,64,768]{2,1,0:T(8,128)(2,1)} %og.1, f32[16,64,768]{2,1,0:T(8,128)} %tu.1, ...), custom_call_target="tpu_custom_call" | custom-call | tf_op jit(solution)/shard_map/pallas_call | solution.py:286
  91.1 1.9 %shard_map.102 = (bf16[16,24,2048]{2,1,0:T(8,128)(2,1)}, bf16[16,24,2048]{2,1,0:T(8,128)(2,1)}, f32[16,24]{1,0:T(8,128)}, f32[16,24]{1,0:T(8,128)}, bf16[2048,128]{1,0:T(8,128)(2,1)}) custom-call(bf16[16,24,2048]{2,1,0:T(8,128)(2,1)S(1)} %get-tuple-element.15.refs_0_, bf16[16,24,2048]{2,1,0:T(8,128)(2,1)S(1)} %get-tuple-element.16.refs_1_, ...), custom_call_target="tpu_custom_call" | custom-call | tf_op jit(solution)/shard_map/pallas_call | solution.py:327

commit v5 on v4

--- a/solution.py
+++ b/solution.py
@@ -145,13 +145,12 @@
     def take_fin(row, at):
         pltpu.make_async_copy(scales.at[at], scales.at[at], fin_recv.at[row]).wait()
 
-    for r in range(NY):
-
+    def take_first(r):
         @pl.when(me != r)
         def _():
             take_fin(r, place(r))
 
-    def post(c):
+    def make(c):
         y, z = lax.rem(2 * c, NY), lax.div(2 * c, NY)
         inv_g = 1.0 / scales[y * nz + z]
         inv_u = 1.0 / scales[(y + 1) * nz + z]
@@ -163,12 +162,18 @@
         for p in range(n):
             send[c, p] = turned[p * wide : (p + 1) * wide, :].astype(jnp.bfloat16)
         recv[c, me] = send[c, me]
+
+    def give(c, k):
+        p = peer_of(k)
+        pltpu.make_async_remote_copy(
+            src_ref=send.at[c, p], dst_ref=recv.at[c, me], send_sem=main_send.at[c], recv_sem=main_recv.at[c],
+            device_id={"zero": p}, device_id_type=MESH,
+        ).start()
+
+    def post(c):
+        make(c)
         for k in offsets:
-            p = peer_of(k)
-            pltpu.make_async_remote_copy(
-                src_ref=send.at[c, p], dst_ref=recv.at[c, me], send_sem=main_send.at[c], recv_sem=main_recv.at[c],
-                device_id={"zero": p}, device_id_type=MESH,
-            ).start()
+            give(c, k)
 
     def send_rows(k):
         at = pl.ds(my_y * nz + 1, nz - 1)
@@ -177,7 +182,11 @@
             device_id={"zero": peer_of(k)}, device_id_type=MESH,
         )
 
+    take_first(0)
+    take_first(1)
     post(0)
+    take_first(2)
+    take_first(3)
     for z in range(1, nz):
 
         @pl.when(my_z != z)
@@ -194,7 +203,11 @@
             at = pl.ds(y * nz + 1, nz - 1)
             pltpu.make_async_copy(scales.at[at], scales.at[at], side_recv.at[y]).wait()
 
-    pl.loop(2, chunks)(post)
+    pl.loop(2, chunks - 10)(post)
+    pl.loop(chunks - 10, chunks)(make)
+    for k in offsets:
+        for c in range(chunks - 10, chunks):
+            give(c, k)
 
     pltpu.make_async_copy(rrecv.at[pl.ds(0, n - 1)], rrecv.at[pl.ds(0, n - 1)], r_recv).wait()
     low = lax.broadcasted_iota(jnp.int32, (half, lanes), 1) < rows

time: 93.2 us -> 91.9 us (0.986)
  Pallas kernels: 92.3 us -> 91.1 us
    pallas_call x1, Pallas kernels: 90.4 us -> 89.2 us  [on_device(): pl.pallas_call(functools.partial(kernel, n, nb), out_shape=tuple((pltpu.V...]
where the time goes in v5:
time: 91.9 us; the launch traced here: 91.7 us
  Pallas kernels  91.1 us (99%)
    pallas_call x1, Pallas kernels, on_device(): pl.pallas_call(functools.partial(kernel, n, nb), out_shape=tuple((pltpu.V...  89.2 us
    pallas_call x1, Pallas kernels, on_device(): pl.pallas_call(store, out_shape=shapes, in_specs=[vmem] * 5, out_specs=(h...  1.88 us

profile of v5, /device:TPU:2, one launch (start us, length us, event | category | flops | bytes accessed | tf_op | source)
XLA Modules:
  0.0 91.7 jit_solution(5695467094773255241)
XLA Ops:
  0.6 89.2 %shard_map.101 = (bf16[16,24,2048]{2,1,0:T(8,128)(2,1)S(1)}, bf16[16,24,2048]{2,1,0:T(8,128)(2,1)S(1)}, f32[16,24]{1,0:T(8,128)S(1)}, f32[16,24]{1,0:T(8,128)S(1)}, bf16[2048,128]{1,0:T(8,128)(2,1)S(1)}) custom-call(f32[16,64,768]{2,1,0:T(8,128)} %tg.1, bf16[16,64,768]{2,1,0:T(8,128)(2,1)} %og.1, f32[16,64,768]{2,1,0:T(8,128)} %tu.1, ...), custom_call_target="tpu_custom_call" | custom-call | tf_op jit(solution)/shard_map/pallas_call | solution.py:299
  89.8 1.9 %shard_map.102 = (bf16[16,24,2048]{2,1,0:T(8,128)(2,1)}, bf16[16,24,2048]{2,1,0:T(8,128)(2,1)}, f32[16,24]{1,0:T(8,128)}, f32[16,24]{1,0:T(8,128)}, bf16[2048,128]{1,0:T(8,128)(2,1)}) custom-call(bf16[16,24,2048]{2,1,0:T(8,128)(2,1)S(1)} %get-tuple-element.15.refs_0_, bf16[16,24,2048]{2,1,0:T(8,128)(2,1)S(1)} %get-tuple-element.16.refs_1_, ...), custom_call_target="tpu_custom_call" | custom-call | tf_op jit(solution)/shard_map/pallas_call | solution.py:340

commit v6 on v5

--- a/solution.py
+++ b/solution.py
@@ -102,7 +102,12 @@
     @pl.loop(1, chunks)
     def _(c):
         largest(c)
-        pass_on(c)
+
+        @pl.when(c > 1)
+        def _():
+            pass_on(c - 1)
+
+    pass_on(chunks - 1)
 
     gath[me] = part[me]
 
@@ -203,7 +208,10 @@
             at = pl.ds(y * nz + 1, nz - 1)
             pltpu.make_async_copy(scales.at[at], scales.at[at], side_recv.at[y]).wait()
 
-    pl.loop(2, chunks - 10)(post)
+    pl.loop(2, chunks - 10)(make)
+    for k in offsets:
+        for c in range(2, chunks - 10):
+            give(c, k)
     pl.loop(chunks - 10, chunks)(make)
     for k in offsets:
         for c in range(chunks - 10, chunks):

time: 91.9 us -> 91.9 us (level)
  no operation moved by 1% of the time
where the time goes in v6:
time: 91.9 us; the launch traced here: 91.8 us
  Pallas kernels  91.2 us (99%)
    pallas_call x1, Pallas kernels, on_device(): pl.pallas_call(functools.partial(kernel, n, nb), out_shape=tuple((pltpu.V...  89.3 us
    pallas_call x1, Pallas kernels, on_device(): pl.pallas_call(store, out_shape=shapes, in_specs=[vmem] * 5, out_specs=(h...  1.88 us

profile of v6, /device:TPU:2, one launch (start us, length us, event | category | flops | bytes accessed | tf_op | source)
XLA Modules:
  0.0 91.8 jit_solution(10718863993488942933)
XLA Ops:
  0.6 89.3 %shard_map.101 = (bf16[16,24,2048]{2,1,0:T(8,128)(2,1)S(1)}, bf16[16,24,2048]{2,1,0:T(8,128)(2,1)S(1)}, f32[16,24]{1,0:T(8,128)S(1)}, f32[16,24]{1,0:T(8,128)S(1)}, bf16[2048,128]{1,0:T(8,128)(2,1)S(1)}) custom-call(f32[16,64,768]{2,1,0:T(8,128)} %tg.1, bf16[16,64,768]{2,1,0:T(8,128)(2,1)} %og.1, f32[16,64,768]{2,1,0:T(8,128)} %tu.1, ...), custom_call_target="tpu_custom_call" | custom-call | tf_op jit(solution)/shard_map/pallas_call | solution.py:307
  89.9 1.9 %shard_map.102 = (bf16[16,24,2048]{2,1,0:T(8,128)(2,1)}, bf16[16,24,2048]{2,1,0:T(8,128)(2,1)}, f32[16,24]{1,0:T(8,128)}, f32[16,24]{1,0:T(8,128)}, bf16[2048,128]{1,0:T(8,128)(2,1)}) custom-call(bf16[16,24,2048]{2,1,0:T(8,128)(2,1)S(1)} %get-tuple-element.15.refs_0_, bf16[16,24,2048]{2,1,0:T(8,128)(2,1)S(1)} %get-tuple-element.16.refs_1_, ...), custom_call_target="tpu_custom_call" | custom-call | tf_op jit(solution)/shard_map/pallas_call | solution.py:348
